TPU v7x, 32 devices: a whole 2x2x4 slice. The times are simulated.
32 devices in a mesh: node: 8 (over z, x), expert: 4 (over y, core).
Axes of the slice: x: 2, y: 2, z: 4, core: 2. Of those that a mesh axis runs over, the one named last changes fastest.
Arguments:
- tokens: bfloat16 [16384, 1024], P(('node', 'expert')), may hold values from -6 to 6
- queries: bfloat16 [16384, 1024], P(('node', 'expert')), may hold values from -6 to 6
- keys: bfloat16 [16384, 1024], P(('node', 'expert')), may hold values from -6 to 6
- values: bfloat16 [16384, 1024], P(('node', 'expert')), may hold values from -12 to 12
- neighbours: int32 [128, 8], P(('node', 'expert')), may hold values from 0 to 127, as said below
- live_bits: int32 [128, 8], P(('node', 'expert')), may hold values from 0 to 1, as said below
- out_proj: bfloat16 [1024, 1024], replicated, may hold values from -0.1875 to 0.1875
- norm_gain: float32 [1024], replicated, may hold values from 0.5 to 1.5
- router: bfloat16 [1024, 32], replicated, may hold values from -0.1875 to 0.1875
- expert: int32 [16384], P(('node', 'expert')), may hold values from 0 to 31, as said below
- slot: int32 [16384], P(('node', 'expert')), may hold values from 0 to 31, as said below
- w_up: bfloat16 [32, 1024, 4096], P(('node', 'expert')), may hold values from -0.1875 to 0.1875
- w_down: bfloat16 [32, 4096, 1024], P(('node', 'expert')), may hold values from -0.09375 to 0.09375
Outputs:
- layer_out: bfloat16 [16384, 1024], P(('node', 'expert'))
Inputs may be any that keep to these rules, and one draw needn't show every extreme that they name: Tile g is held by device g // 4 in node-major order. neighbours[g, 0] is g itself; every listed tile is held by g's device or by the device one step before or after it along node with the same expert index (wrapping around); entry 1 is always one step before and entry 2 one step after. `live_bits`: entry 0 of every row is 1. Within the 512 tokens of one device, no two tokens share both expert and slot; some expert takes all 32 slots of every device. See expert: pairs (expert, slot) are distinct within one device's tokens.
All inputs are finite; a program needn't handle non-finite values.
Results may differ from a plain program's by a relative error of at most 0.0049.
Values may be sent and summed in bfloat16 or wider, within the bound.
A program may use at most 192 MiB of HBM per device.

v0:
```python
import jax
import jax.numpy as jnp
from jax import lax
from jax.sharding import PartitionSpec as P

D = 1024
HEADS = 16
HEAD_DIM = 64
TILE = 128
NB = 8
score_scale = 0.125


def extended(shard, sides, width):
    for axis, dim in sides:
        size, length = (lax.axis_size(axis), shard.shape[dim])
        up = [(i, (i + 1) % size) for i in range(size)]
        down = [(j, i) for i, j in up]
        last = lax.slice_in_dim(shard, length - width, length, axis=dim)
        leading = lax.slice_in_dim(shard, 0, width, axis=dim)
        before = lax.ppermute(last, axis, up)
        after = lax.ppermute(leading, axis, down)
        shard = jnp.concatenate([before, shard, after], axis=dim)
    return shard


def shards(
    tokens,
    queries,
    keys,
    values,
    neighbours,
    live_bits,
    out_proj,
    norm_gain,
    router,
    expert,
    slot,
    w_up,
    w_down,
):
    tok_dev = tokens.shape[0]
    tiles_dev = tok_dev // TILE
    experts = router.shape[1]
    cap = 2 * tok_dev // experts
    both = jnp.concatenate([keys, values], axis=1)
    widened = extended(both, (("node", 0),), tok_dev)
    window_tiles = widened.reshape(3 * tiles_dev, TILE, 2 * D)
    my_node = lax.axis_index("node")
    node_count = lax.axis_size("node")
    column_count = lax.axis_size("expert")
    owner_node = neighbours // tiles_dev // column_count
    offset = (owner_node - my_node + node_count) % node_count
    block_of = jnp.where(offset == 0, 1, jnp.where(offset == 1, 2, 0))
    position = block_of * tiles_dev + neighbours % tiles_dev
    gathered = window_tiles[position]
    near_keys = gathered[..., :D].reshape(tiles_dev, NB * TILE, HEADS, HEAD_DIM)
    near_values = gathered[..., D:].reshape(tiles_dev, NB * TILE, HEADS, HEAD_DIM)
    query_tiles = queries.reshape(tiles_dev, TILE, HEADS, HEAD_DIM)
    scores = (
        jnp.einsum("tqhd,tkhd->thqk", query_tiles, near_keys, preferred_element_type=jnp.float32)
        * score_scale
    )
    visible = jnp.repeat(live_bits, TILE, axis=1) > 0
    masked = jnp.where(visible[:, None, None, :], scores, -jnp.inf)
    peak = jnp.max(masked, axis=-1, keepdims=True)
    weights = jnp.exp(masked - peak)
    weights = (weights / jnp.sum(weights, axis=-1, keepdims=True)).astype(jnp.bfloat16)
    mixed = jnp.einsum("thqk,tkhd->tqhd", weights, near_values, preferred_element_type=jnp.float32)
    attn = mixed.reshape(tok_dev, D).astype(jnp.bfloat16)
    hidden = tokens.astype(jnp.float32) + jnp.dot(
        attn, out_proj, preferred_element_type=jnp.float32
    )
    spread = jnp.mean(hidden * hidden, axis=-1, keepdims=True)
    normed = (hidden * lax.rsqrt(spread + 1e-06) * norm_gain[None, :]).astype(jnp.bfloat16)
    logits = jnp.dot(normed, router, preferred_element_type=jnp.float32)
    columns = lax.iota(jnp.int32, experts)
    chosen = jnp.sum(jnp.where(columns[None, :] == expert[:, None], logits, 0.0), axis=-1)
    gate = jax.nn.sigmoid(chosen)
    slot_cell = expert * cap + slot
    one_hot = (lax.iota(jnp.int32, experts * cap)[:, None] == slot_cell[None, :]).astype(
        jnp.bfloat16
    )
    outgoing = jnp.dot(one_hot, normed, preferred_element_type=jnp.float32).astype(jnp.bfloat16)
    up_matrix = w_up[0]
    down_matrix = w_down[0]
    block = lax.all_to_all(
        outgoing.reshape(experts, 1, cap, D),
        ("node", "expert"),
        split_axis=0,
        concat_axis=1,
        tiled=True,
    )
    token_rows = block.reshape(-1, D)
    lifted = jnp.dot(token_rows, up_matrix, preferred_element_type=jnp.float32)
    lifted = jax.nn.gelu(lifted, approximate=True).astype(jnp.bfloat16)
    result = jnp.dot(lifted, down_matrix, preferred_element_type=jnp.float32).astype(jnp.bfloat16)
    returned = lax.all_to_all(
        result.reshape(block.shape), ("node", "expert"), split_axis=1, concat_axis=0, tiled=True
    )
    flat_back = returned.reshape(experts * cap, D)
    expert_out = jnp.einsum("ct,cd->td", one_hot, flat_back, preferred_element_type=jnp.float32)
    layer_out = hidden + gate[:, None] * expert_out
    return layer_out.astype(jnp.bfloat16)


def solution(mesh):
    in_specs = (
        P(("node", "expert"), None),
        P(("node", "expert"), None),
        P(("node", "expert"), None),
        P(("node", "expert"), None),
        P(("node", "expert"), None),
        P(("node", "expert"), None),
        P(),
        P(),
        P(),
        P(("node", "expert")),
        P(("node", "expert")),
        P(("node", "expert"), None, None),
        P(("node", "expert"), None, None),
    )
    out_specs = P(("node", "expert"), None)
    return jax.shard_map(shards, mesh=mesh, in_specs=in_specs, out_specs=out_specs, check_vma=False)
```

profile of v0, /device:TPU:0, one launch (start us, length us, event | category | flops | bytes accessed | tf_op | source)
XLA Modules:
  0.0 354.2 jit_solution(12946120193367616058)
XLA Ops:
  0.0 2.5 constant_dynamic-update-slice_fusion.1
  2.5 2.3 constant_dynamic-update-slice_fusion
  4.8 6.0 %collective-permute-start.1 = (bf16[512,2048]{1,0:T(8,128)(2,1)}, bf16[512,2048]{1,0:T(8,128)(2,1)}, u32[]{:S(2)}, u32[]{:S(2)}) collective-permute-start(bf16[512,2048]{1,0:T(8,128)(2,1)} %constant_dynamic-update-slice_fusion), channel_id=1, source_target_pairs={{4,0},{8,4},{12,8},{16,12},{20,16},{24,20},{28,24},{0,28},{5,1},{9... | collective-permute-start | bytes 6291464 | tf_op jit(solution)/shard_map/ppermute | solution.py:22
  12.3 4.0 %reshape.79 = bf16[4,128,16,64]{3,2,1,0:T(8,128)(2,1)} reshape(bf16[512,1024]{1,0:T(8,128)(2,1)} %param.14) | data formatting | bytes 2097152 | tf_op jit(solution)/shard_map/reshape | solution.py:59
  16.4 82.2 %collective-permute-done.1 = bf16[512,2048]{1,0:T(8,128)(2,1)} collective-permute-done((bf16[512,2048]{1,0:T(8,128)(2,1)}, bf16[512,2048]{1,0:T(8,128)(2,1)}, u32[]{:S(2)}, u32[]{:S(2)}) %collective-permute-start.1) | collective-permute-done | bytes 2097184 | tf_op jit(solution)/shard_map/ppermute | solution.py:22
  98.8 5.9 %pad_maximum_fusion = bf16[1536,2048]{1,0:T(8,128)(2,1)} fusion(bf16[512,2048]{1,0:T(8,128)(2,1)} %collective-permute-done.1, bf16[512,2048]{1,0:T(8,128)(2,1)} %constant_dynamic-update-slice_fusion, bf16[512,2048]{1,0:T(8,128)(2,1)} %collective-permute-done), kind=kLoop, calls=%fused_computation.28 | loop fusion | flops 18874368 | bytes 12582912 | tf_op jit(solution)/shard_map/concatenate | solution.py:23
  104.7 10.1 %gather_fusion = bf16[32,128,2048]{2,1,0:T(8,128)(2,1)} fusion(bf16[12,128,2048]{2,1,0:T(8,128)(2,1)} %bitcast.64, s32[1024]{0:T(1024)S(1)} %pad_clamp_fusion), kind=kCustom, calls=%fused_computation | custom fusion | bytes 33554560 | tf_op jit(solution)/shard_map/gather | solution.py:56
  114.7 11.9 %fusion.66 = (bf16[4,8,128,1024]{3,2,1,0:T(8,128)(2,1)}, bf16[4,8,128,1024]{3,2,1,0:T(8,128)(2,1)}) fusion(bf16[4,8,128,2048]{3,2,1,0:T(8,128)(2,1)} %bitcast.65), kind=kLoop, calls=%fused_computation.88 | loop fusion | bytes 33554432 | tf_op jit(solution)/shard_map/slice | solution.py:57
  126.6 12.3 %copy.22 = bf16[4,8,128,1024]{2,1,3,0:T(8,128)(2,1)} copy(bf16[4,8,128,1024]{3,2,1,0:T(8,128)(2,1)} %get-tuple-element.6) | data formatting | bytes 16777216 | tf_op jit(solution)/shard_map/slice | solution.py:58
  138.9 13.3 %reshape.62 = bf16[4,1024,16,64]{1,3,2,0:T(8,128)(2,1)} reshape(bf16[4,8,128,1024]{2,1,3,0:T(8,128)(2,1)} %copy.22) | data formatting | bytes 16777216 | tf_op jit(solution)/shard_map/reshape | solution.py:58
  152.2 12.3 %copy.23 = bf16[4,8,128,1024]{2,1,3,0:T(8,128)(2,1)} copy(bf16[4,8,128,1024]{3,2,1,0:T(8,128)(2,1)} %get-tuple-element.5) | data formatting | bytes 16777216 | tf_op jit(solution)/shard_map/slice | solution.py:57
  164.6 13.3 %reshape.63 = bf16[4,1024,16,64]{1,3,2,0:T(8,128)(2,1)} reshape(bf16[4,8,128,1024]{2,1,3,0:T(8,128)(2,1)} %copy.23) | data formatting | bytes 16777216 | tf_op jit(solution)/shard_map/reshape | solution.py:57
  177.8 18.8 %fusion.67 = (f32[4,16,128]{2,1,0:T(8,128)S(1)}, f32[4,16,128,1024]{2,3,1,0:T(8,128)}) fusion(pred[4,1024]{1,0:T(4,128)(4,1)S(1)} %bitcast.69, bf16[4,1024,16,64]{1,3,2,0:T(8,128)(2,1)} %reshape.63, bf16[4,128,16,64]{3,2,1,0:T(8,128)(2,1)} %reshape.79), kind=kOutput, calls=%fused_computation.89 | convolution fusion | flops 1107297280 | bytes 43028480 | tf_op jit(solution)/shard_map/sub | solution.py:67
  196.6 14.6 %fusion.47 = bf16[4,128,16,64]{1,3,2,0:T(8,128)(2,1)S(1)} fusion(bf16[4,1024,16,64]{1,3,2,0:T(8,128)(2,1)} %reshape.62, f32[4,16,128,1024]{2,3,1,0:T(8,128)} %get-tuple-element.8, f32[4,16,128]{2,1,0:T(8,128)S(1)} %get-tuple-element.7), kind=kOutput, calls=%fused_computation.43 | convolution fusion | flops 1091043328 | bytes 43024384 | tf_op jit(solution)/shard_map/thqk,tkhd->tqhd/dot_general | solution.py:69
  211.3 0.9 copy.27
  212.2 2.6 multiply_reduce_fusion
  214.8 1.3 copy-done.2
  216.1 1.4 fusion.38
  217.5 54.7 %all_to_all.8 = bf16[32,1,32,1024]{3,2,1,0:T(8,128)(2,1)S(1)} all-to-all(bf16[32,1,32,1024]{3,2,1,0:T(8,128)(2,1)S(1)} %bitcast.68), channel_id=1, replica_groups=mesh['node'=8,'expert'=4] {'node','expert'}, dimensions={0} | all-to-all | bytes 4194304 | tf_op jit(solution)/shard_map/all_to_all | solution.py:87
  272.2 25.0 %fusion.29 = bf16[1024,1024]{1,0:T(8,128)(2,1)} fusion(bf16[1,4096,1024]{2,1,0:T(8,128)(2,1)} %param.25, bf16[1024,1024]{1,0:T(8,128)(2,1)S(1)} %bitcast.67, bf16[1,1024,4096]{2,1,0:T(8,128)(2,1)} %param.24), kind=kOutput, calls=%fused_computation.37 | convolution fusion | flops 17218666496 | bytes 20971520 | tf_op jit(solution)/shard_map/dot_general | solution.py:97
  297.2 3.8 %all-to-all-start.1 = ((bf16[1,32,32,1024]{3,2,0,1:T(8,128)(2,1)}), bf16[1,32,32,1024]{3,2,0,1:T(8,128)(2,1)}, u32[]{:S(2)}, u32[]{:S(2)}) async-start(bf16[1,32,32,1024]{3,2,0,1:T(8,128)(2,1)} %bitcast.10), calls=%async_computation.1 | async-start | bytes 4194304 | tf_op jit(solution)/shard_map/all_to_all | solution.py:98
  301.0 2.2 fusion.48
  303.3 46.4 %all-to-all-done.1 = bf16[1,32,32,1024]{3,2,0,1:T(8,128)(2,1)} async-done(((bf16[1,32,32,1024]{3,2,0,1:T(8,128)(2,1)}), bf16[1,32,32,1024]{3,2,0,1:T(8,128)(2,1)}, u32[]{:S(2)}, u32[]{:S(2)}) %all-to-all-start.1) | async-done | bytes 2097184 | tf_op jit(solution)/shard_map/all_to_all | solution.py:98
  349.7 4.5 %add_convert_fusion = bf16[512,1024]{1,0:T(8,128)(2,1)} fusion(f32[512,1024]{1,0:T(8,128)} %copy-done.2, bf16[1024,1024]{1,0:T(8,128)(2,1)} %bitcast.11, s32[512]{0:T(512)S(1)} %multiply_add_fusion, f32[512]{0:T(512)S(1)} %add_divide_fusion), kind=kOutput, calls=%fused_computation.30 | convolution fusion | flops 1075838976 | bytes 5246976 | tf_op jit(solution)/shard_map/ct,cd->td/dot_general | solution.py:102
  (26 shorter events, 1.8 us)
Async XLA Ops:
  0.0 212.2 %copy-start = (bf16[1024,1024]{1,0:T(8,128)(2,1)S(1)}, bf16[1024,1024]{1,0:T(8,128)(2,1)}, u32[]{:S(2)}) copy-start(bf16[1024,1024]{1,0:T(8,128)(2,1)} %param.19) | copy-start | bytes 6291460
  0.0 16.4 %copy-start.7 = (s32[512]{0:T(512)S(1)}, s32[512]{0:T(512)}, u32[]{:S(2)}) copy-start(s32[512]{0:T(512)} %param.23) | copy-start | bytes 6148
  0.0 16.4 %copy-start.4 = (s32[512]{0:T(512)S(1)}, s32[512]{0:T(512)}, u32[]{:S(2)}) copy-start(s32[512]{0:T(512)} %param.22) | copy-start | bytes 6148
  4.8 93.9 %collective-permute-start.1 = (bf16[512,2048]{1,0:T(8,128)(2,1)}, bf16[512,2048]{1,0:T(8,128)(2,1)}, u32[]{:S(2)}, u32[]{:S(2)}) collective-permute-start(bf16[512,2048]{1,0:T(8,128)(2,1)} %constant_dynamic-update-slice_fusion), channel_id=1, source_target_pairs={{4,0},{8,4},{12,8},{16,12},{20,16},{24,20},{28,24},{0,28},{5,1},{9... | collective-permute-start | bytes 6291464 | tf_op jit(solution)/shard_map/ppermute | solution.py:22
  10.8 88.0 %collective-permute-start = (bf16[512,2048]{1,0:T(8,128)(2,1)}, bf16[512,2048]{1,0:T(8,128)(2,1)}, u32[]{:S(2)}, u32[]{:S(2)}) collective-permute-start(bf16[512,2048]{1,0:T(8,128)(2,1)} %constant_dynamic-update-slice_fusion), channel_id=1, source_target_pairs={{0,4},{4,8},{8,12},{12,16},{16,20},{20,24},{24,28},{28,0},{1,5},{5... | collective-permute-start | bytes 6291464 | tf_op jit(solution)/shard_map/ppermute | solution.py:21
  211.3 4.9 %copy-start.6 = (f32[1024]{0:T(1024)S(1)}, f32[1024]{0:T(1024)}, u32[]{:S(2)}) copy-start(f32[1024]{0:T(1024)} %param.20) | copy-start | bytes 12292
  214.8 1.3 copy-start.2
  272.2 28.8 %copy-start.3 = (bf16[1024,32]{0,1:T(8,128)(2,1)S(1)}, bf16[1024,32]{0,1:T(8,128)(2,1)}, u32[]{:S(2)}) copy-start(bf16[1024,32]{0,1:T(8,128)(2,1)} %param.21) | copy-start | bytes 196612
  272.2 28.8 %copy-start.5 = (s32[512]{0:T(512)S(1)}, s32[512]{0:T(512)}, u32[]{:S(2)}) copy-start(s32[512]{0:T(512)} %param.22) | copy-start | bytes 6148
  297.2 52.5 %all-to-all-start.1 = ((bf16[1,32,32,1024]{3,2,0,1:T(8,128)(2,1)}), bf16[1,32,32,1024]{3,2,0,1:T(8,128)(2,1)}, u32[]{:S(2)}, u32[]{:S(2)}) async-start(bf16[1,32,32,1024]{3,2,0,1:T(8,128)(2,1)} %bitcast.10), calls=%async_computation.1 | async-start | bytes 4194304 | tf_op jit(solution)/shard_map/all_to_all | solution.py:98
  301.0 53.2 %copy-start.1 = (bf16[1024,1024]{1,0:T(8,128)(2,1)S(1)}, bf16[1024,1024]{1,0:T(8,128)(2,1)}, u32[]{:S(2)}) copy-start(bf16[1024,1024]{1,0:T(8,128)(2,1)} %param.19) | copy-start | bytes 6291460
where the time goes:
time: 356 us; the launch traced here: 354 us
  waiting for transfers between devices  129 us (36%)
  local copies, waits for them, and re-layouts  84.3 us (24%)
  matrix products  69.1 us (19%)
  blocking collectives  54.7 us (15%)
  starting transfers between devices  9.8 us (3%)
  other arithmetic  7.34 us (2%)
    ppermute x1, waiting for transfers between devices, extended(): after = lax.ppermute(leading, axis, down)  82.2 us
    all_to_all x1, blocking collectives, shards(): lax.all_to_all(outgoing.reshape(experts, 1, cap, D), ('node', 'expert'),...  54.7 us
    all_to_all x1, waiting for transfers between devices, shards(): lax.all_to_all(result.reshape(block.shape), ('node', 'expert'), split_axi...  46.4 us
    dot_general x1, matrix products, shards(): jnp.dot(lifted, down_matrix, preferred_element_type=jnp.float32)  25 us
    slice x2, local copies, waits for them, and re-layouts, shards(): near_keys = gathered[..., :D].reshape(tiles_dev, NB * TILE, HEADS, HEAD_DIM)  24.2 us
    sub x1, matrix products, shards(): weights = jnp.exp(masked - peak)  18.8 us
    dot_general x1, matrix products, shards(): jnp.einsum('thqk,tkhd->tqhd', weights, near_values, preferred_element_typ...  14.6 us
    reshape x1, local copies, waits for them, and re-layouts, shards(): gathered[..., D:].reshape(tiles_dev, NB * TILE, HEADS, HEAD_DIM)  13.3 us
  transfers between devices with their start and end apart: 3, of which 3 were waited for; matrix products, arithmetic and copies ran while one was open for 2% of the time, Pallas kernels for 0%

commit v1 on v0

--- a/solution.py
+++ b/solution.py
@@ -9,6 +9,13 @@
 TILE = 128
 NB = 8
 score_scale = 0.125
+
+
+def trade_parts(x, axis, split, join):
+    size = lax.axis_size(axis)
+    blocks = jnp.stack(jnp.split(x, size, axis=split), axis=0)
+    blocks = lax.all_to_all(blocks, axis, split_axis=0, concat_axis=0)
+    return jnp.concatenate(blocks, axis=join)
 
 
 def extended(shard, sides, width):
@@ -84,13 +91,7 @@
     outgoing = jnp.dot(one_hot, normed, preferred_element_type=jnp.float32).astype(jnp.bfloat16)
     up_matrix = w_up[0]
     down_matrix = w_down[0]
-    block = lax.all_to_all(
-        outgoing.reshape(experts, 1, cap, D),
-        ("node", "expert"),
-        split_axis=0,
-        concat_axis=1,
-        tiled=True,
-    )
+    block = trade_parts(outgoing.reshape(experts, 1, cap, D), ("node", "expert"), 0, 1)
     token_rows = block.reshape(-1, D)
     lifted = jnp.dot(token_rows, up_matrix, preferred_element_type=jnp.float32)
     lifted = jax.nn.gelu(lifted, approximate=True).astype(jnp.bfloat16)

time: 356 us -> 354 us (level)
  waiting for transfers between devices: 129 us -> 134 us
  local copies, waits for them, and re-layouts: 84.3 us -> 80.7 us
  transfers between devices with their start and end apart: 3 -> 3, of which waited for: 3 -> 3; matrix products, arithmetic and copies ran while one was open for 2% -> 1% of each run, Pallas kernels for 0% -> 0%
where the time goes in v1:
time: 354 us; the launch traced here: 352 us
  waiting for transfers between devices  134 us (38%)
  local copies, waits for them, and re-layouts  80.7 us (23%)
  matrix products  66.9 us (19%)
  blocking collectives  54.8 us (15%)
  starting transfers between devices  9.8 us (3%)
  other arithmetic  5.97 us (2%)
    ppermute x1, waiting for transfers between devices, extended(): after = lax.ppermute(leading, axis, down)  85.2 us
    all_to_all x1, blocking collectives, trade_parts(): blocks = lax.all_to_all(blocks, axis, split_axis=0, concat_axis=0)  54.8 us
    all_to_all x1, waiting for transfers between devices, shards(): lax.all_to_all(result.reshape(block.shape), ('node', 'expert'), split_axi...  48.1 us
    dot_general x1, matrix products, shards(): jnp.dot(lifted, down_matrix, preferred_element_type=jnp.float32)  25.5 us
    slice x2, local copies, waits for them, and re-layouts, shards(): near_keys = gathered[..., :D].reshape(tiles_dev, NB * TILE, HEADS, HEAD_DIM)  24.2 us
    sub x1, matrix products, shards(): weights = jnp.exp(masked - peak)  18.8 us
    dot_general x1, matrix products, shards(): jnp.einsum('thqk,tkhd->tqhd', weights, near_values, preferred_element_typ...  14.6 us
    reshape x1, local copies, waits for them, and re-layouts, shards(): gathered[..., D:].reshape(tiles_dev, NB * TILE, HEADS, HEAD_DIM)  13.3 us
  transfers between devices with their start and end apart: 3, of which 3 were waited for; matrix products, arithmetic and copies ran while one was open for 1% of the time, Pallas kernels for 0%

profile of v1, /device:TPU:0, one launch (start us, length us, event | category | flops | bytes accessed | tf_op | source)
XLA Modules:
  0.0 352.1 jit_solution(10449588060041755676)
XLA Ops:
  0.0 2.5 constant_dynamic-update-slice_fusion.1
  2.5 1.1 constant_dynamic-update-slice_fusion
  3.6 6.0 %collective-permute-start.1 = (bf16[512,2048]{1,0:T(8,128)(2,1)}, bf16[512,2048]{1,0:T(8,128)(2,1)}, u32[]{:S(2)}, u32[]{:S(2)}) collective-permute-start(bf16[512,2048]{1,0:T(8,128)(2,1)} %constant_dynamic-update-slice_fusion), channel_id=1, source_target_pairs={{4,0},{8,4},{12,8},{16,12},{20,16},{24,20},{28,24},{0,28},{5,1},{9... | collective-permute-start | bytes 6291464 | tf_op jit(solution)/shard_map/ppermute | solution.py:29
  9.8 2.4 reshape.132
  12.2 85.2 %collective-permute-done.1 = bf16[512,2048]{1,0:T(8,128)(2,1)} collective-permute-done((bf16[512,2048]{1,0:T(8,128)(2,1)}, bf16[512,2048]{1,0:T(8,128)(2,1)}, u32[]{:S(2)}, u32[]{:S(2)}) %collective-permute-start.1) | collective-permute-done | bytes 2097184 | tf_op jit(solution)/shard_map/ppermute | solution.py:29
  97.6 5.9 %pad_maximum_fusion = bf16[1536,2048]{1,0:T(8,128)(2,1)} fusion(bf16[512,2048]{1,0:T(8,128)(2,1)} %collective-permute-done.1, bf16[512,2048]{1,0:T(8,128)(2,1)} %constant_dynamic-update-slice_fusion, bf16[512,2048]{1,0:T(8,128)(2,1)} %collective-permute-done), kind=kLoop, calls=%fused_computation.28 | loop fusion | flops 18874368 | bytes 12582912 | tf_op jit(solution)/shard_map/concatenate | solution.py:30
  103.5 10.1 %gather_fusion = bf16[32,128,2048]{2,1,0:T(8,128)(2,1)} fusion(bf16[12,128,2048]{2,1,0:T(8,128)(2,1)} %bitcast.189, s32[1024]{0:T(1024)S(1)} %pad_clamp_fusion), kind=kCustom, calls=%fused_computation | custom fusion | bytes 33554560 | tf_op jit(solution)/shard_map/gather | solution.py:63
  113.6 11.9 %fusion.66 = (bf16[4,8,128,1024]{3,2,1,0:T(8,128)(2,1)}, bf16[4,8,128,1024]{3,2,1,0:T(8,128)(2,1)}) fusion(bf16[4,8,128,2048]{3,2,1,0:T(8,128)(2,1)} %bitcast.190), kind=kLoop, calls=%fused_computation.152 | loop fusion | bytes 33554432 | tf_op jit(solution)/shard_map/slice | solution.py:64
  125.4 12.3 %copy.22 = bf16[4,8,128,1024]{2,1,3,0:T(8,128)(2,1)} copy(bf16[4,8,128,1024]{3,2,1,0:T(8,128)(2,1)} %get-tuple-element.6) | data formatting | bytes 16777216 | tf_op jit(solution)/shard_map/slice | solution.py:65
  137.7 13.3 %reshape.117 = bf16[4,1024,16,64]{1,3,2,0:T(8,128)(2,1)} reshape(bf16[4,8,128,1024]{2,1,3,0:T(8,128)(2,1)} %copy.22) | data formatting | bytes 16777216 | tf_op jit(solution)/shard_map/reshape | solution.py:65
  151.1 12.3 %copy.23 = bf16[4,8,128,1024]{2,1,3,0:T(8,128)(2,1)} copy(bf16[4,8,128,1024]{3,2,1,0:T(8,128)(2,1)} %get-tuple-element.5) | data formatting | bytes 16777216 | tf_op jit(solution)/shard_map/slice | solution.py:64
  163.4 13.3 %reshape.118 = bf16[4,1024,16,64]{1,3,2,0:T(8,128)(2,1)} reshape(bf16[4,8,128,1024]{2,1,3,0:T(8,128)(2,1)} %copy.23) | data formatting | bytes 16777216 | tf_op jit(solution)/shard_map/reshape | solution.py:64
  176.7 18.8 %fusion.67 = (f32[4,16,128]{2,1,0:T(8,128)S(1)}, f32[4,16,128,1024]{2,3,1,0:T(8,128)}) fusion(pred[4,1024]{1,0:T(4,128)(4,1)S(1)} %bitcast.194, bf16[4,1024,16,64]{1,3,2,0:T(8,128)(2,1)} %reshape.118, bf16[4,128,16,64]{3,2,1,0:T(8,128)(2,1)} %reshape.132), kind=kOutput, calls=%fused_computation.153 | convolution fusion | flops 1107297280 | bytes 43028480 | tf_op jit(solution)/shard_map/sub | solution.py:74
  195.5 14.6 %fusion.47 = bf16[4,128,16,64]{1,3,2,0:T(8,128)(2,1)S(1)} fusion(bf16[4,1024,16,64]{1,3,2,0:T(8,128)(2,1)} %reshape.117, f32[4,16,128,1024]{2,3,1,0:T(8,128)} %get-tuple-element.8, f32[4,16,128]{2,1,0:T(8,128)S(1)} %get-tuple-element.7), kind=kOutput, calls=%fused_computation.43 | convolution fusion | flops 1091043328 | bytes 43024384 | tf_op jit(solution)/shard_map/thqk,tkhd->tqhd/dot_general | solution.py:76
  210.2 0.9 copy.27
  211.1 0.3 copy-done.6
  211.4 1.4 multiply_reduce_fusion
  212.8 1.4 fusion.38
  214.7 54.8 %all_to_all.14 = bf16[32,1,1,32,1024]{4,3,2,1,0:T(8,128)(2,1)} all-to-all(bf16[32,1,1,32,1024]{4,3,2,1,0:T(8,128)(2,1)S(1)} %constant_dynamic-update-slice_fusion.2), channel_id=1, replica_groups=mesh['node'=8,'expert'=4] {'node','expert'}, dimensions={0} | all-to-all | bytes 4194304 | tf_op jit(solution)/shard_map/all_to_all | solution.py:17
  269.4 25.5 %fusion.29 = bf16[1024,1024]{1,0:T(8,128)(2,1)} fusion(bf16[1,4096,1024]{2,1,0:T(8,128)(2,1)} %param.25, bf16[1024,1024]{1,0:T(8,128)(2,1)} %bitcast.193, bf16[1,1024,4096]{2,1,0:T(8,128)(2,1)} %param.24), kind=kOutput, calls=%fused_computation.37 | convolution fusion | flops 17218666496 | bytes 20971520 | tf_op jit(solution)/shard_map/dot_general | solution.py:98
  295.0 3.8 %all-to-all-start.1 = ((bf16[1,32,32,1024]{3,2,0,1:T(8,128)(2,1)}), bf16[1,32,32,1024]{3,2,0,1:T(8,128)(2,1)}, u32[]{:S(2)}, u32[]{:S(2)}) async-start(bf16[1,32,32,1024]{3,2,0,1:T(8,128)(2,1)} %bitcast.192), calls=%async_computation.1 | async-start | bytes 4194304 | tf_op jit(solution)/shard_map/all_to_all | solution.py:99
  298.8 0.5 fusion.48
  299.3 48.1 %all-to-all-done.1 = bf16[1,32,32,1024]{3,2,0,1:T(8,128)(2,1)} async-done(((bf16[1,32,32,1024]{3,2,0,1:T(8,128)(2,1)}), bf16[1,32,32,1024]{3,2,0,1:T(8,128)(2,1)}, u32[]{:S(2)}, u32[]{:S(2)}) %all-to-all-start.1) | async-done | bytes 2097184 | tf_op jit(solution)/shard_map/all_to_all | solution.py:99
  347.5 4.6 %add_convert_fusion = bf16[512,1024]{1,0:T(8,128)(2,1)} fusion(f32[512,1024]{1,0:T(8,128)} %copy-done.2, bf16[1024,1024]{1,0:T(8,128)(2,1)} %bitcast.41, s32[512]{0:T(512)S(1)} %multiply_add_fusion, f32[512]{0:T(512)S(1)} %add_divide_fusion), kind=kOutput, calls=%fused_computation.30 | convolution fusion | flops 1075838976 | bytes 5246976 | tf_op jit(solution)/shard_map/ct,cd->td/dot_general | solution.py:103
  (70 shorter events, 0.7 us)
Async XLA Ops:
  0.0 211.1 %copy-start = (bf16[1024,1024]{1,0:T(8,128)(2,1)S(1)}, bf16[1024,1024]{1,0:T(8,128)(2,1)}, u32[]{:S(2)}) copy-start(bf16[1024,1024]{1,0:T(8,128)(2,1)} %param.19) | copy-start | bytes 6291460
  0.0 2.5 copy-start.5
  0.0 9.6 %copy-start.13 = (s32[4,8]{1,0:T(4,128)S(1)}, s32[4,8]{1,0:T(4,128)}, u32[]{:S(2)}) copy-start(s32[4,8]{1,0:T(4,128)} %param.17) | copy-start | bytes 388
  0.0 9.7 %copy-start.12 = (s32[4,8]{1,0:T(4,128)S(1)}, s32[4,8]{1,0:T(4,128)}, u32[]{:S(2)}) copy-start(s32[4,8]{1,0:T(4,128)} %param.18) | copy-start | bytes 388
  0.0 9.8 %copy-start.4 = (bf16[512,1024]{1,0:T(8,128)(2,1)S(1)}, bf16[512,1024]{1,0:T(8,128)(2,1)}, u32[]{:S(2)}) copy-start(bf16[512,1024]{1,0:T(8,128)(2,1)} %param.14) | copy-start | bytes 3145732
  3.6 8.6 %copy-start.8 = (s32[512]{0:T(512)S(1)}, s32[512]{0:T(512)}, u32[]{:S(2)}) copy-start(s32[512]{0:T(512)} %param.22) | copy-start | bytes 6148
  3.6 8.6 %copy-start.11 = (s32[512]{0:T(512)S(1)}, s32[512]{0:T(512)}, u32[]{:S(2)}) copy-start(s32[512]{0:T(512)} %param.23) | copy-start | bytes 6148
  3.6 93.9 %collective-permute-start.1 = (bf16[512,2048]{1,0:T(8,128)(2,1)}, bf16[512,2048]{1,0:T(8,128)(2,1)}, u32[]{:S(2)}, u32[]{:S(2)}) collective-permute-start(bf16[512,2048]{1,0:T(8,128)(2,1)} %constant_dynamic-update-slice_fusion), channel_id=1, source_target_pairs={{4,0},{8,4},{12,8},{16,12},{20,16},{24,20},{28,24},{0,28},{5,1},{9... | collective-permute-start | bytes 6291464 | tf_op jit(solution)/shard_map/ppermute | solution.py:29
  9.6 88.0 %collective-permute-start = (bf16[512,2048]{1,0:T(8,128)(2,1)}, bf16[512,2048]{1,0:T(8,128)(2,1)}, u32[]{:S(2)}, u32[]{:S(2)}) collective-permute-start(bf16[512,2048]{1,0:T(8,128)(2,1)} %constant_dynamic-update-slice_fusion), channel_id=1, source_target_pairs={{0,4},{4,8},{8,12},{12,16},{16,20},{20,24},{24,28},{28,0},{1,5},{5... | collective-permute-start | bytes 6291464 | tf_op jit(solution)/shard_map/ppermute | solution.py:28
  210.2 1.2 copy-start.6
  211.4 1.4 copy-start.10
  212.8 1.4 copy-start.2
  295.0 3.8 %copy-start.3 = (f32[512,1024]{1,0:T(8,128)S(1)}, f32[512,1024]{1,0:T(8,128)}, u32[]{:S(2)}) copy-start(f32[512,1024]{1,0:T(8,128)} %copy-done.2) | copy-start | bytes 6291460
  295.0 3.8 %copy-start.7 = (bf16[1024,32]{0,1:T(8,128)(2,1)S(1)}, bf16[1024,32]{0,1:T(8,128)(2,1)}, u32[]{:S(2)}) copy-start(bf16[1024,32]{0,1:T(8,128)(2,1)} %param.21) | copy-start | bytes 196612
  295.0 3.8 %copy-start.9 = (s32[512]{0:T(512)S(1)}, s32[512]{0:T(512)}, u32[]{:S(2)}) copy-start(s32[512]{0:T(512)} %param.22) | copy-start | bytes 6148
  295.0 52.5 %all-to-all-start.1 = ((bf16[1,32,32,1024]{3,2,0,1:T(8,128)(2,1)}), bf16[1,32,32,1024]{3,2,0,1:T(8,128)(2,1)}, u32[]{:S(2)}, u32[]{:S(2)}) async-start(bf16[1,32,32,1024]{3,2,0,1:T(8,128)(2,1)} %bitcast.192), calls=%async_computation.1 | async-start | bytes 4194304 | tf_op jit(solution)/shard_map/all_to_all | solution.py:99
  347.5 4.6 %copy-start.1 = (bf16[1024,1024]{1,0:T(8,128)(2,1)S(1)}, bf16[1024,1024]{1,0:T(8,128)(2,1)}, u32[]{:S(2)}) copy-start(bf16[1024,1024]{1,0:T(8,128)(2,1)} %param.19) | copy-start | bytes 6291460
